TPU v7x, 32 devices: a whole 2x2x4 slice. The times are simulated.
32 devices in a mesh: ep: 8 (over y, x, core), tp: 4 (over z).
Axes of the slice: x: 2, y: 2, z: 4, core: 2. Of those that a mesh axis runs over, the one named last changes fastest.
Arguments:
- tokens: bfloat16 [1024, 2048], P('ep', 'tp'), may hold values from -6 to 6
- routing: int32 [1024, 8], P('ep'), may hold values from 0 to 31, all different within a row; in each aligned block of 128 rows (0 to 127, 128 to 255, ...) at most 64 rows name the same one
- gate_fixed: int32 [1024, 8], P('ep'), may hold values from 1 to 65535
- gate_weight: bfloat16 [32, 2048, 768], P('ep', 'tp'), may hold values from -0.125 to 0.125
- up_weight: bfloat16 [32, 2048, 768], P('ep', 'tp'), may hold values from -0.1875 to 0.1875
- down_weight: bfloat16 [32, 2048, 768], P('ep', 'tp'), may hold values from -0.21875 to 0.21875
Outputs:
- layer_out: bfloat16 [1024, 2048], P('ep', 'tp')
Inputs may be any that keep to these rules, and one draw needn't show every extreme that they name: `routing`: each token names 8 different experts. In each aligned block of 128 tokens (the tokens of one index of ep) no expert is named by more than 64 tokens, and in some blocks one expert is named by exactly 64.
All inputs are finite; a program needn't handle non-finite values.
Results may differ from a plain program's by a relative error of at most 0.0057.
Values may be sent and summed in bfloat16 or wider, within the bound.
A program may use at most 64 MiB of HBM per device.

v0:
```python
import jax
import jax.numpy as jnp
from jax import lax
from jax.sharding import PartitionSpec as P


def slot_numbers(routing, experts, capacity):
    token_rows, top_count = routing.shape
    flat_ids = routing.reshape(-1)
    one_hot = (flat_ids[:, None] == jnp.arange(experts, dtype=jnp.int32)[None, :]).astype(jnp.int32)
    earlier = jnp.cumsum(one_hot, axis=0) - one_hot
    position = jnp.sum(earlier * one_hot, axis=1)
    return (flat_ids * capacity + position).reshape(token_rows, top_count)


def on_device(tokens, routing, gate_fixed, gate_weight, up_weight, down_weight):
    ep_count = lax.axis_size("ep")
    tp_count = lax.axis_size("tp")
    local_experts, feature_share, hidden_width = gate_weight.shape
    experts = local_experts * ep_count
    token_rows, top_count = routing.shape
    capacity = max(2, token_rows * top_count * 2 // experts)
    slot_count = experts * capacity
    unit_share = hidden_width // tp_count
    slot_index = slot_numbers(routing, experts, capacity)
    token_ids = jnp.repeat(jnp.arange(token_rows, dtype=jnp.int32), top_count)
    owners = jnp.zeros((slot_count,), jnp.int32).at[slot_index.reshape(-1)].set(token_ids)
    outgoing = jnp.take(tokens, owners, axis=0)
    arrived = lax.all_to_all(outgoing, "ep", split_axis=0, concat_axis=0, tiled=True)
    gate_split, up_split = (
        lax.all_to_all(gate_weight, "tp", split_axis=2, concat_axis=1, tiled=True),
        lax.all_to_all(up_weight, "tp", split_axis=2, concat_axis=1, tiled=True),
    )
    portion = lax.all_gather(arrived, "tp", axis=1, tiled=True)
    width = portion.shape[1]
    pieces = portion.reshape(ep_count, local_experts, capacity, width)
    gate_part = jnp.einsum("secd,edf->fsec", pieces, gate_split, preferred_element_type=jnp.float32)
    up_part = jnp.einsum("secd,edf->fsec", pieces, up_split, preferred_element_type=jnp.float32)
    gate_acts = gate_part.reshape(unit_share, slot_count)
    up_acts = up_part.reshape(unit_share, slot_count)
    hidden_share = (jax.nn.silu(gate_acts) * up_acts).astype(jnp.bfloat16)
    portion = lax.all_gather(hidden_share, "tp", axis=0, tiled=True)
    length = portion.shape[0]
    units = portion.reshape(length, ep_count, local_experts, capacity)
    expert_sum = jnp.einsum(
        "fsec,edf->secd", units, down_weight, preferred_element_type=jnp.float32
    )
    expert_out = expert_sum.astype(jnp.bfloat16).reshape(slot_count, feature_share)
    returned = lax.all_to_all(expert_out, "ep", split_axis=0, concat_axis=0, tiled=True)
    picked = jnp.take(returned, slot_index.reshape(-1), axis=0).reshape(
        token_rows, top_count, feature_share
    )
    scales = gate_fixed.astype(jnp.float32) / 65536.0
    mixed = jnp.sum(picked.astype(jnp.float32) * scales[:, :, None], axis=1)
    return mixed.astype(jnp.bfloat16)


def solution(mesh):
    in_specs = (
        P("ep", "tp"),
        P("ep", None),
        P("ep", None),
        P("ep", "tp", None),
        P("ep", "tp", None),
        P("ep", "tp", None),
    )
    out_specs = P("ep", "tp")
    return jax.shard_map(
        on_device, mesh=mesh, in_specs=in_specs, out_specs=out_specs, check_vma=False
    )
```

profile of v0, /device:TPU:1, one launch (start us, length us, event | category | flops | bytes accessed | tf_op | source)
XLA Modules:
  0.0 494.6 jit_solution(4922828496650510369)
XLA Ops:
  6.5 0.0 copy-start
  6.5 0.0 copy-start.1
  6.5 0.0 all-gather.3.cloned.1.call-start
  6.5 0.9 copy.47
  7.5 0.1 eq.26
  7.6 0.7 reshape.95
  8.3 1.3 broadcast_multiply_fusion
  9.6 9.0 %reduce-window.6 = s32[32,8,128]{2,1,0:T(8,128)S(1)} reduce-window(s32[32,8,128]{2,1,0:T(8,128)S(1)} %fusion.30, s32[]{:T(128)} %constant.26.clone.1), window={size=1x1x128 pad=0_0x0_0x127_0}, to_apply=%region_0.0 | reduce-window | flops 4161536 | bytes 262148 | tf_op jit(solution)/shard_map/reduce-window
  18.6 0.1 slice.12
  18.7 0.1 copy.49
  18.8 0.1 copy.50
  18.9 0.1 broadcast_add_fusion
  19.0 0.8 copy.53
  19.8 0.1 mul.40
  19.9 0.1 reshape.122
  20.0 0.7 fusion.29
  20.8 4.3 scatter_custom_fusion
  25.1 0.0 copy-done.1
  25.1 9.2 %gather_fusion = bf16[2048,512]{1,0:T(8,128)(2,1)} fusion(bf16[128,512]{1,0:T(8,128)(2,1)S(1)} %copy-done.1, s32[2048]{0:T(1024)S(1)} %fusion.31), kind=kCustom, calls=%fused_computation | custom fusion | bytes 4202496 | tf_op jit(solution)/shard_map/jit(_take)/gather | solution.py:28
  34.3 1.8 broadcast_select_fusion
  36.1 30.5 %all_to_all.57 = bf16[8,256,512]{2,1,0:T(8,128)(2,1)} all-to-all(bf16[8,256,512]{2,1,0:T(8,128)(2,1)S(1)} %broadcast_select_fusion), channel_id=1, replica_groups=mesh['ep'=8,'tp'=4] {'ep'}, dimensions={0} | all-to-all | bytes 4194304 | tf_op jit(solution)/shard_map/all_to_all | solution.py:29
  66.6 0.0 all-gather.3.cloned.1.call-update
  66.6 6.2 %copy.54 = bf16[4,512,768]{1,0,2:T(4,128)(2,1)} copy(bf16[4,512,768]{2,1,0:T(8,128)(2,1)} %param.9) | data formatting | bytes 6291456 | tf_op args[3]
  72.8 4.8 all-to-all-start.1
  77.6 6.2 %copy.59 = bf16[4,512,768]{1,0,2:T(4,128)(2,1)} copy(bf16[4,512,768]{2,1,0:T(8,128)(2,1)} %param.10) | data formatting | bytes 6291456 | tf_op args[4]
  83.8 149.2 %all-to-all-done.1 = bf16[4,512,768]{1,0,2:T(4,128)(2,1)} async-done(((bf16[4,512,768]{1,0,2:T(4,128)(2,1)}), bf16[4,512,768]{1,0,2:T(4,128)(2,1)}, u32[]{:S(2)}, u32[]{:S(2)}) %all-to-all-start.1) | async-done | bytes 3145760 | tf_op jit(solution)/shard_map/all_to_all | solution.py:31
  233.0 4.7 all-to-all-start.2
  237.7 0.0 all-gather.5.cloned.1.call-start
  237.7 2.5 copy.55
  240.2 4.1 copy.56
  244.3 6.2 %reshape.127 = bf16[4,2048,192,1]{1,2,0,3:T(8,128)(2,1)} reshape(bf16[4,4,512,192]{2,1,3,0:T(4,128)(2,1)} %copy.56) | data formatting | bytes 6291456 | tf_op jit(solution)/shard_map/all_to_all | solution.py:31
  250.5 99.5 %all-to-all-done.2 = bf16[4,512,768]{1,0,2:T(4,128)(2,1)} async-done(((bf16[4,512,768]{1,0,2:T(4,128)(2,1)}), bf16[4,512,768]{1,0,2:T(4,128)(2,1)}, u32[]{:S(2)}, u32[]{:S(2)}) %all-to-all-start.2) | async-done | bytes 3145760 | tf_op jit(solution)/shard_map/all_to_all | solution.py:32
  350.0 2.5 copy.60
  352.5 4.1 copy.61
  356.6 6.1 %reshape.128 = bf16[4,2048,192,1]{1,2,0,3:T(8,128)(2,1)} reshape(bf16[4,4,512,192]{2,1,3,0:T(4,128)(2,1)} %copy.61) | data formatting | bytes 6291456 | tf_op jit(solution)/shard_map/all_to_all | solution.py:32
  362.6 0.0 all-gather.3.cloned.1.call-done
  362.6 0.0 copy-start.5
  362.6 6.8 %fusion.17 = f32[192,8,4,64]{0,3,1,2:T(8,128)S(1)} fusion(bf16[4,2048,192,1]{1,2,0,3:T(8,128)(2,1)} %reshape.127, bf16[8,4,64,2048]{3,2,1,0:T(8,128)(2,1)} %bitcast.91), kind=kOutput, calls=%fused_computation.22 | convolution fusion | flops 1610612736 | bytes 13107200 | tf_op jit(solution)/shard_map/secd,edf->fsec/dot_general | solution.py:37
  369.4 0.0 copy-start.2
  369.4 0.2 copy.58
  369.6 0.0 copy-done.5
  369.6 1.7 copy-done.2
  371.3 2.3 fusion.22
  373.6 0.2 copy.63
  373.9 1.6 fusion.9
  375.5 2.2 copy.64
  377.7 0.0 all-gather.5.cloned.1.call-update
  377.7 62.1 %all-gather.5.cloned.1.call-done = bf16[768,2048]{1,0:T(8,128)(2,1)} async-done(((bf16[192,2048]{1,0:T(8,128)(2,1)}), bf16[768,2048]{1,0:T(8,128)(2,1)}) %all-gather.5.cloned.1.call-update) | async-done | bytes 3145744 | tf_op jit(solution)/shard_map/all_gather | solution.py:42
  439.9 4.7 copy.65
  444.5 0.0 copy-done
  444.5 3.7 convert_bitcast_fusion
  448.3 1.5 copy.67
  449.8 0.0 copy-start.3
  449.8 0.0 copy-start.4
  449.8 5.2 %all-to-all-start.3 = ((bf16[8,256,512]{2,1,0:T(8,128)(2,1)}), bf16[8,256,512]{2,1,0:T(8,128)(2,1)}, u32[]{:S(2)}, u32[]{:S(2)}) async-start(bf16[8,256,512]{2,1,0:T(8,128)(2,1)} %bitcast.84), calls=%async_computation.3 | async-start | bytes 4194304 | tf_op jit(solution)/shard_map/all_to_all | solution.py:49
  455.0 0.1 reduce_sum.23
  455.1 0.0 copy-done.3
  455.1 0.1 copy.52
  455.3 0.0 copy-done.4
  455.3 0.1 copy.68
  455.4 22.7 %all-to-all-done.3 = bf16[8,256,512]{2,1,0:T(8,128)(2,1)} async-done(((bf16[8,256,512]{2,1,0:T(8,128)(2,1)}), bf16[8,256,512]{2,1,0:T(8,128)(2,1)}, u32[]{:S(2)}, u32[]{:S(2)}) %all-to-all-start.3) | async-done | bytes 2097184 | tf_op jit(solution)/shard_map/all_to_all | solution.py:49
  478.1 7.0 %gather_fusion.1 = bf16[1024,512]{1,0:T(8,128)(2,1)} fusion(bf16[2048,512]{1,0:T(8,128)(2,1)} %bitcast.22, s32[1024]{0:T(1024)S(1)} %broadcast_clamp_fusion), kind=kCustom, calls=%fused_computation.1 | custom fusion | bytes 2101248 | tf_op jit(solution)/shard_map/jit(_take)/gather | solution.py:50
  485.1 2.7 multiply_reduce_fusion
  (12 shorter events, 0.2 us)
Async XLA Ops:
  6.5 438.0 %copy-start = (bf16[4,512,768]{2,1,0:T(8,128)(2,1)S(1)}, bf16[4,512,768]{2,1,0:T(8,128)(2,1)}, u32[]{:S(2)}) copy-start(bf16[4,512,768]{2,1,0:T(8,128)(2,1)} %param.11) | copy-start | bytes 9437188
  6.5 18.6 %copy-start.1 = (bf16[128,512]{1,0:T(8,128)(2,1)S(1)}, bf16[128,512]{1,0:T(8,128)(2,1)}, u32[]{:S(2)}) copy-start(bf16[128,512]{1,0:T(8,128)(2,1)} %param.6) | copy-start | bytes 393220
  6.5 356.1 %all-gather.3.cloned.1.call-start = ((), (), s32[]{:S(2)}) async-start(), calls=%async_computation.4 | async-start | bytes 10485760 | tf_op jit(solution)/shard_map/all_gather | solution.py:34
  72.8 160.2 %all-to-all-start.1 = ((bf16[4,512,768]{1,0,2:T(4,128)(2,1)}), bf16[4,512,768]{1,0,2:T(4,128)(2,1)}, u32[]{:S(2)}, u32[]{:S(2)}) async-start(bf16[4,512,768]{1,0,2:T(4,128)(2,1)} %copy.54), calls=%async_computation.1 | async-start | bytes 6291456 | tf_op jit(solution)/shard_map/all_to_all | solution.py:31
  233.0 117.0 %all-to-all-start.2 = ((bf16[4,512,768]{1,0,2:T(4,128)(2,1)}), bf16[4,512,768]{1,0,2:T(4,128)(2,1)}, u32[]{:S(2)}, u32[]{:S(2)}) async-start(bf16[4,512,768]{1,0,2:T(4,128)(2,1)} %copy.59), calls=%async_computation.2 | async-start | bytes 6291456 | tf_op jit(solution)/shard_map/all_to_all | solution.py:32
  237.7 202.2 %all-gather.5.cloned.1.call-start = ((), (), s32[]{:S(2)}) async-start(), calls=%async_computation.5 | async-start | bytes 3932160 | tf_op jit(solution)/shard_map/all_gather | solution.py:42
  362.6 7.0 %copy-start.5 = (bf16[2048,2048]{1,0:T(8,128)(2,1)S(1)}, bf16[2048,2048]{1,0:T(8,128)(2,1)}, u32[]{:S(2)}) copy-start(bf16[2048,2048]{1,0:T(8,128)(2,1)} %all-gather.3.cloned.1.call-done) | copy-start | bytes 25165828
  369.4 1.9 copy-start.2
  449.8 5.3 %copy-start.3 = (s32[128,8]{0,1:T(8,128)S(1)}, s32[128,8]{0,1:T(8,128)}, u32[]{:S(2)}) copy-start(s32[128,8]{0,1:T(8,128)} %param.7) | copy-start | bytes 12292
  449.8 5.5 %copy-start.4 = (s32[128,8]{0,1:T(8,128)S(1)}, s32[128,8]{0,1:T(8,128)}, u32[]{:S(2)}) copy-start(s32[128,8]{0,1:T(8,128)} %param.8) | copy-start | bytes 12292
  449.8 28.3 %all-to-all-start.3 = ((bf16[8,256,512]{2,1,0:T(8,128)(2,1)}), bf16[8,256,512]{2,1,0:T(8,128)(2,1)}, u32[]{:S(2)}, u32[]{:S(2)}) async-start(bf16[8,256,512]{2,1,0:T(8,128)(2,1)} %bitcast.84), calls=%async_computation.3 | async-start | bytes 4194304 | tf_op jit(solution)/shard_map/all_to_all | solution.py:49
Sparse Core Ops, SparseCore 0:
  66.7 280.1 all-gather.2
  377.9 61.9 all-gather.4
where the time goes:
time: 500 us; the launch traced here: 495 us
  waiting for transfers between devices  334 us (67%)
  local copies, waits for them, and re-layouts  72.2 us (14%)
  blocking collectives  30.5 us (6%)
  other arithmetic  17.3 us (3%)
  starting transfers between devices  14.7 us (3%)
  between operations  13.6 us (3%)
  matrix products  12.8 us (3%)
    all_to_all x1, waiting for transfers between devices, on_device(): lax.all_to_all(gate_weight, 'tp', split_axis=2, concat_axis=1, tiled=True)  149 us
    all_to_all x1, waiting for transfers between devices, on_device(): lax.all_to_all(up_weight, 'tp', split_axis=2, concat_axis=1, tiled=True)  99.5 us
    all_gather x1, waiting for transfers between devices, on_device(): portion = lax.all_gather(hidden_share, 'tp', axis=0, tiled=True)  62.1 us
    all_to_all x1, blocking collectives, on_device(): lax.all_to_all(outgoing, 'ep', split_axis=0, concat_axis=0, tiled=True)  30.5 us
    all_to_all x1, waiting for transfers between devices, on_device(): lax.all_to_all(expert_out, 'ep', split_axis=0, concat_axis=0, tiled=True)  22.7 us
    unnamed x15, local copies, waits for them, and re-layouts  15.1 us
    all_to_all x3, local copies, waits for them, and re-layouts, on_device(): lax.all_to_all(gate_weight, 'tp', split_axis=2, concat_axis=1, tiled=True)  12.7 us
    all_to_all x3, local copies, waits for them, and re-layouts, on_device(): lax.all_to_all(up_weight, 'tp', split_axis=2, concat_axis=1, tiled=True)  12.6 us
  transfers between devices with their start and end apart: 5, of which 4 were waited for; matrix products, arithmetic and copies ran while one was open for 8% of the time, Pallas kernels for 0%

commit v1 on v0

v1 whole, which is shorter than its diff:
```python
import functools

import jax
import jax.numpy as jnp
from jax import lax
from jax.experimental import pallas as pl
from jax.experimental.pallas import tpu as pltpu
from jax.sharding import PartitionSpec as P

MESH = pl.DeviceIdType.MESH
SKEW = 2


def layer_kernel(
    nep, n, local, cap, top,
    tok_ref, meta_ref, gw_hbm, uw_hbm, dw_hbm,
    out_ref,
    gw, uw, dw, tok_all, meta_all,
    ra, rb, ha, hb, pg, pu, acc, out_send, out_recv,
    w_sem, tok_s, tok_r, meta_s, meta_r,
    ra_s, ra_r, rb_s, rb_r, ha_s, ha_r, hb_s, hb_r, out_s, out_r,
):
    me = lax.axis_index("ep")
    z = lax.axis_index("tp")
    half = local // 2
    chunks = nep * half
    rows = tok_ref.shape[0]
    width = gw.shape[2]
    zl = lax.rem(z + n - 1, n)
    zr = lax.rem(z + 1, n)

    weight_copies = [
        pltpu.make_async_copy(src, dst, w_sem.at[i])
        for i, (src, dst) in enumerate(((gw_hbm, gw), (uw_hbm, uw), (dw_hbm, dw)))
    ]
    for copy in weight_copies:
        copy.start()

    barrier = pltpu.get_barrier_semaphore()

    def greet(j, carry):
        pl.semaphore_signal(
            barrier, inc=1, device_id={"ep": lax.rem(me + j, nep)}, device_id_type=MESH
        )
        return carry

    lax.fori_loop(1, nep, greet, 0)

    for side in (zl, zr):
        pl.semaphore_signal(barrier, inc=1, device_id={"tp": side}, device_id_type=MESH)
    pl.semaphore_wait(barrier, nep + 1)

    def remote(src, dst, s, r, device):
        return pltpu.make_async_remote_copy(
            src_ref=src, dst_ref=dst, send_sem=s, recv_sem=r,
            device_id=device, device_id_type=MESH,
        )

    def tok_copy(j):
        to = {"ep": lax.rem(me - j + nep, nep)}
        return remote(tok_ref, tok_all.at[j], tok_s.at[j], tok_r.at[j], to)

    def meta_copy(j):
        to = {"ep": lax.rem(me - j + nep, nep)}
        return remote(meta_ref, meta_all.at[j], meta_s.at[j], meta_r.at[j], to)

    def out_copy(j):
        to = {"ep": lax.rem(me + j, nep)}
        return remote(out_send.at[j], out_recv.at[j], out_s.at[j], out_r.at[j], to)

    def ra_copy(k):
        return remote(ra.at[k], ra.at[k], ra_s.at[k], ra_r.at[k], {"tp": zl})

    def rb_copy(k):
        return remote(rb.at[k], rb.at[k], rb_s.at[k], rb_r.at[k], {"tp": zr})

    def ha_copy(k):
        return remote(ha.at[k], ha.at[k], ha_s.at[k], ha_r.at[k], {"tp": zr})

    def hb_copy(k):
        return remote(hb.at[k], hb.at[k], hb_s.at[k], hb_r.at[k], {"tp": zl})

    def send_tokens(j, carry):
        meta_copy(j).start()
        tok_copy(j).start()
        return carry

    lax.fori_loop(1, nep, send_tokens, 0)
    tok_all[0] = tok_ref[...]
    meta_all[0] = meta_ref[...]

    def clear(j, carry):
        acc[j] = jnp.zeros(acc.shape[1:], acc.dtype)
        return carry

    lax.fori_loop(0, nep, clear, 0)
    for copy in weight_copies:
        copy.wait()

    before = (
        lax.broadcasted_iota(jnp.int32, (rows, rows), 0)
        < lax.broadcasted_iota(jnp.int32, (rows, rows), 1)
    ).astype(jnp.bfloat16)
    slot_id = lax.broadcasted_iota(jnp.int32, (cap, rows), 0).astype(jnp.float32)

    def selection(j, e):
        named = meta_all[j, :top, :] == me * local + e
        chosen = jnp.sum(named.astype(jnp.float32), axis=0, keepdims=True)
        wide = jnp.broadcast_to(chosen, (16, rows)).astype(jnp.bfloat16)
        position = jnp.dot(wide, before, preferred_element_type=jnp.float32)[:1]
        hit = jnp.where(chosen > 0.5, position, -1.0)
        return named, slot_id == hit

    def gates(j, named, picked):
        values = meta_all[j, top:, :].astype(jnp.float32) / 65536.0
        row = jnp.sum(jnp.where(named, values, 0.0), axis=0, keepdims=True)
        return jnp.sum(jnp.where(picked, row, 0.0), axis=1, keepdims=True)

    def inside(k):
        return jnp.logical_and(k >= 0, k < chunks)

    def partial_stage(k, first_expert, buf, copy, has_source, is_last, hidden):
        @pl.when(inside(k))
        def _():
            j = k // half
            e = first_expert + k % half
            _, picked = selection(j, e)
            x = jnp.dot(
                picked.astype(jnp.bfloat16), tok_all[j], preferred_element_type=jnp.float32
            ).astype(jnp.bfloat16)
            pg[...] = jnp.dot(x, gw[e], preferred_element_type=jnp.float32)
            pu[...] = jnp.dot(x, uw[e], preferred_element_type=jnp.float32)

            @pl.when(has_source)
            def _():
                copy(k).wait_recv()
                pg[...] += buf[k, :, :width].astype(jnp.float32)
                pu[...] += buf[k, :, width:].astype(jnp.float32)

            @pl.when(jnp.logical_not(is_last))
            def _():
                buf[k, :, :width] = pg[...].astype(jnp.bfloat16)
                buf[k, :, width:] = pu[...].astype(jnp.bfloat16)
                copy(k).start()

            @pl.when(is_last)
            def _():
                v = pg[...]
                hidden[k] = (v / (1.0 + jnp.exp(-v)) * pu[...]).astype(jnp.bfloat16)

    def hidden_stage(k, first_expert, hidden, copy, has_source, is_last):
        @pl.when(inside(k))
        def _():
            @pl.when(has_source)
            def _():
                copy(k).wait_recv()

            @pl.when(jnp.logical_not(is_last))
            def _():
                copy(k).start()

            j = k // half
            e = first_expert + k % half
            named, picked = selection(j, e)
            result = lax.dot_general(
                hidden[k], dw[e], (((1,), (1,)), ((), ())), preferred_element_type=jnp.float32
            )
            scaled = (result * gates(j, named, picked)).astype(jnp.bfloat16)
            acc[j] += lax.dot_general(
                picked.astype(jnp.bfloat16), scaled, (((0,), (0,)), ((), ())),
                preferred_element_type=jnp.float32,
            )

    turn = SKEW * (n - 1)
    from_right = SKEW * (n - 1 - z)
    from_left = SKEW * z

    def step(t, carry):
        k_first = t - jnp.minimum(from_left, from_right)

        @pl.when(jnp.logical_and(inside(k_first), k_first % half == 0))
        def _():
            j = k_first // half

            @pl.when(j > 0)
            def _():
                meta_copy(j).wait_recv()
                tok_copy(j).wait_recv()

        partial_stage(t - from_right, 0, ra, ra_copy, z < n - 1, z == 0, ha)
        partial_stage(t - from_left, half, rb, rb_copy, z > 0, z == n - 1, hb)
        hidden_stage(t - turn - from_left, 0, ha, ha_copy, z > 0, z == n - 1)
        hidden_stage(t - turn - from_right, half, hb, hb_copy, z < n - 1, z == 0)
        k_done = t - turn - jnp.maximum(from_left, from_right)

        @pl.when(jnp.logical_and(inside(k_done), k_done % half == half - 1))
        def _():
            j = k_done // half

            @pl.when(j > 0)
            def _():
                out_send[j] = acc[j].astype(jnp.bfloat16)
                out_copy(j).start()

        return carry

    lax.fori_loop(0, chunks + 2 * turn, step, 0)

    def finish_chunk(k, carry):
        @pl.when(z > 0)
        def _():
            ra_copy(k).wait_send()
            hb_copy(k).wait_send()

        @pl.when(z < n - 1)
        def _():
            rb_copy(k).wait_send()
            ha_copy(k).wait_send()

        return carry

    lax.fori_loop(0, chunks, finish_chunk, 0)

    def finish_block(j, carry):
        tok_copy(j).wait_send()
        meta_copy(j).wait_send()
        out_copy(j).wait_recv()
        acc[0] += out_recv[j].astype(jnp.float32)
        out_copy(j).wait_send()
        return carry

    lax.fori_loop(1, nep, finish_block, 0)
    out_ref[...] = acc[0].astype(jnp.bfloat16)


def on_device(nep, n, tokens, routing, gate_fixed, gate_weight, up_weight, down_weight):
    local, share, width = gate_weight.shape
    rows, top = routing.shape
    cap = max(2, rows * top * 2 // (local * nep))
    chunks = nep * (local // 2)
    meta = jnp.concatenate([routing.T, gate_fixed.T], axis=0)
    bf16, f32 = jnp.bfloat16, jnp.float32
    dma = pltpu.SemaphoreType.DMA
    vmem = pl.BlockSpec(memory_space=pltpu.VMEM)
    hbm = pl.BlockSpec(memory_space=pl.ANY)
    return pl.pallas_call(
        functools.partial(layer_kernel, nep, n, local, cap, top),
        out_shape=jax.ShapeDtypeStruct((rows, share), bf16),
        in_specs=[vmem, vmem, hbm, hbm, hbm],
        out_specs=vmem,
        scratch_shapes=[
            pltpu.VMEM((local, share, width), bf16),
            pltpu.VMEM((local, share, width), bf16),
            pltpu.VMEM((local, share, width), bf16),
            pltpu.VMEM((nep, rows, share), bf16),
            pltpu.VMEM((nep, 2 * top, rows), jnp.int32),
            pltpu.VMEM((chunks, cap, 2 * width), bf16),
            pltpu.VMEM((chunks, cap, 2 * width), bf16),
            pltpu.VMEM((chunks, cap, width), bf16),
            pltpu.VMEM((chunks, cap, width), bf16),
            pltpu.VMEM((cap, width), f32),
            pltpu.VMEM((cap, width), f32),
            pltpu.VMEM((nep, rows, share), f32),
            pltpu.VMEM((nep, rows, share), bf16),
            pltpu.VMEM((nep, rows, share), bf16),
            dma((3,)),
            dma((nep,)), dma((nep,)), dma((nep,)), dma((nep,)),
            dma((chunks,)), dma((chunks,)), dma((chunks,)), dma((chunks,)),
            dma((chunks,)), dma((chunks,)), dma((chunks,)), dma((chunks,)),
            dma((nep,)), dma((nep,)),
        ],
        compiler_params=pltpu.CompilerParams(
            collective_id=0, has_side_effects=True, vmem_limit_bytes=60 * 1024 * 1024
        ),
    )(tokens, meta, gate_weight, up_weight, down_weight)


def solution(mesh):
    in_specs = (
        P("ep", "tp"),
        P("ep", None),
        P("ep", None),
        P("ep", "tp", None),
        P("ep", "tp", None),
        P("ep", "tp", None),
    )
    body = functools.partial(on_device, mesh.shape["ep"], mesh.shape["tp"])
    return jax.shard_map(
        body, mesh=mesh, in_specs=in_specs, out_specs=P("ep", "tp"), check_vma=False
    )
```

time: 500 us -> 141 us (0.28)
  waiting for transfers between devices: 334 us -> 0 us
  Pallas kernels: 0 us -> 138 us
  local copies, waits for them, and re-layouts: 72.2 us -> 1.57 us
  blocking collectives: 30.5 us -> 0 us
  other arithmetic: 17.3 us -> 1.3 us
  starting transfers between devices: 14.7 us -> 0 us
  between operations: 13.6 us -> 0.01 us
  matrix products: 12.8 us -> 0 us
    all_to_all x3 -> x0, waiting for transfers between devices: 271 us -> none  [the longest x1 149 us: on_device(): lax.all_to_all(gate_weight, 'tp', split_axis=2, concat_axis=1, tiled=True)]
    pallas_call x0 -> x1, Pallas kernels: none -> 138 us  [on_device(): pl.pallas_call(functools.partial(layer_kernel, nep, n, local, cap, top),...]
    all_gather x2 -> x0, waiting for transfers between devices: 62.1 us -> none  [the longest x1 62.1 us: on_device(): portion = lax.all_gather(hidden_share, 'tp', axis=0, tiled=True)]
    all_to_all x1 -> x0, blocking collectives: 30.5 us -> none  [on_device(): lax.all_to_all(outgoing, 'ep', split_axis=0, concat_axis=0, tiled=True)]
    all_to_all x6 -> x0, local copies, waits for them, and re-layouts: 25.4 us -> none  [the longest x3 12.7 us: on_device(): lax.all_to_all(gate_weight, 'tp', split_axis=2, concat_axis=1, tiled=True)]
    gather x2 -> x0, local copies, waits for them, and re-layouts: 16.2 us -> none  [the longest x1 9.2 us: on_device(): outgoing = jnp.take(tokens, owners, axis=0)]
    all_to_all x3 -> x0, starting transfers between devices: 14.7 us -> none  [the longest x1 5.18 us: on_device(): lax.all_to_all(expert_out, 'ep', split_axis=0, concat_axis=0, tiled=True)]
    unnamed x15 -> x1, local copies, waits for them, and re-layouts: 15.1 us -> 1.57 us
  transfers between devices with their start and end apart: 5 -> 0, of which waited for: 4 -> 0; matrix products, arithmetic and copies ran while one was open for 8% -> 0% of each run, Pallas kernels for 0% -> 0%
where the time goes in v1:
time: 141 us; the launch traced here: 140 us
  Pallas kernels  138 us (98%)
  local copies, waits for them, and re-layouts  1.57 us (1%)
    pallas_call x1, Pallas kernels, on_device(): pl.pallas_call(functools.partial(layer_kernel, nep, n, local, cap, top),...  138 us

profile of v1, /device:TPU:1, one launch (start us, length us, event | category | flops | bytes accessed | tf_op | source)
XLA Modules:
  0.0 140.4 jit_solution(859579016597282521)
XLA Ops:
  0.0 1.3 pad_add_fusion.meta_ref
  1.3 137.6 %shard_map.64 = bf16[128,512]{1,0:T(8,128)(2,1)} custom-call(bf16[128,512]{1,0:T(8,128)(2,1)} %tok_ref.1, s32[16,128]{1,0:T(8,128)} %pad_add_fusion.meta_ref, bf16[4,512,768]{2,1,0:T(8,128)(2,1)} %gw_hbm.1, bf16[4,512,768]{2,1,0:T(8,128)(2,1)} %uw_hbm.1, bf16[4,512,768]{2,1,0:T(8,128)(2,1)} %dw_hbm.1), custom_call_target="tpu_custom_call" | custom-call | tf_op jit(solution)/shard_map/pallas_call | solution.py:246
  138.9 1.6 %copy.8 = bf16[128,512]{1,0:T(8,128)(2,1)} copy(bf16[128,512]{1,0:T(8,128)(2,1)} %shard_map.64) | data formatting | bytes 262144

commit v2 on v1

--- a/solution.py
+++ b/solution.py
@@ -29,12 +29,15 @@
     zl = lax.rem(z + n - 1, n)
     zr = lax.rem(z + 1, n)
 
-    weight_copies = [
-        pltpu.make_async_copy(src, dst, w_sem.at[i])
-        for i, (src, dst) in enumerate(((gw_hbm, gw), (uw_hbm, uw), (dw_hbm, dw)))
-    ]
-    for copy in weight_copies:
-        copy.start()
+    def weight_copy(i, e):
+        src, dst = ((gw_hbm, gw), (uw_hbm, uw), (dw_hbm, dw))[i]
+        return pltpu.make_async_copy(src.at[e], dst.at[e], w_sem.at[i, e])
+
+    for i in ((0, 1), (2,)):
+        for e in range(half):
+            for first in (0, half):
+                for which in i:
+                    weight_copy(which, first + e).start()
 
     barrier = pltpu.get_barrier_semaphore()
 
@@ -94,9 +97,6 @@
         return carry
 
     lax.fori_loop(0, nep, clear, 0)
-    for copy in weight_copies:
-        copy.wait()
-
     before = (
         lax.broadcasted_iota(jnp.int32, (rows, rows), 0)
         < lax.broadcasted_iota(jnp.int32, (rows, rows), 1)
@@ -124,6 +124,12 @@
         def _():
             j = k // half
             e = first_expert + k % half
+
+            @pl.when(j == 0)
+            def _():
+                weight_copy(0, e).wait()
+                weight_copy(1, e).wait()
+
             _, picked = selection(j, e)
             x = jnp.dot(
                 picked.astype(jnp.bfloat16), tok_all[j], preferred_element_type=jnp.float32
@@ -161,13 +167,23 @@
 
             j = k // half
             e = first_expert + k % half
+
+            @pl.when(j == 0)
+            def _():
+                weight_copy(2, e).wait()
+
             named, picked = selection(j, e)
             result = lax.dot_general(
                 hidden[k], dw[e], (((1,), (1,)), ((), ())), preferred_element_type=jnp.float32
             )
-            scaled = (result * gates(j, named, picked)).astype(jnp.bfloat16)
+            scaled = result * gates(j, named, picked)
+            high = scaled.astype(jnp.bfloat16)
+            low = (scaled - high.astype(jnp.float32)).astype(jnp.bfloat16)
+            spread = picked.astype(jnp.bfloat16)
             acc[j] += lax.dot_general(
-                picked.astype(jnp.bfloat16), scaled, (((0,), (0,)), ((), ())),
+                jnp.concatenate([spread, spread], axis=0),
+                jnp.concatenate([high, low], axis=0),
+                (((0,), (0,)), ((), ())),
                 preferred_element_type=jnp.float32,
             )
 
@@ -263,7 +279,7 @@
             pltpu.VMEM((nep, rows, share), f32),
             pltpu.VMEM((nep, rows, share), bf16),
             pltpu.VMEM((nep, rows, share), bf16),
-            dma((3,)),
+            dma((3, local)),
             dma((nep,)), dma((nep,)), dma((nep,)), dma((nep,)),
             dma((chunks,)), dma((chunks,)), dma((chunks,)), dma((chunks,)),
             dma((chunks,)), dma((chunks,)), dma((chunks,)), dma((chunks,)),

time: 141 us -> 139 us (0.986)
  Pallas kernels: 138 us -> 136 us
    pallas_call x1, Pallas kernels: 138 us -> 136 us  [on_device(): pl.pallas_call(functools.partial(layer_kernel, nep, n, local, cap, top),...]
where the time goes in v2:
time: 139 us; the launch traced here: 138 us
  Pallas kernels  136 us (98%)
  local copies, waits for them, and re-layouts  1.57 us (1%)
    pallas_call x1, Pallas kernels, on_device(): pl.pallas_call(functools.partial(layer_kernel, nep, n, local, cap, top),...  136 us

profile of v2, /device:TPU:1, one launch (start us, length us, event | category | flops | bytes accessed | tf_op | source)
XLA Modules:
  0.0 138.4 jit_solution(16980456115657084440)
XLA Ops:
  0.0 1.3 pad_add_fusion.meta_ref
  1.3 135.5 %shard_map.64 = bf16[128,512]{1,0:T(8,128)(2,1)} custom-call(bf16[128,512]{1,0:T(8,128)(2,1)} %tok_ref.1, s32[16,128]{1,0:T(8,128)} %pad_add_fusion.meta_ref, bf16[4,512,768]{2,1,0:T(8,128)(2,1)} %gw_hbm.1, bf16[4,512,768]{2,1,0:T(8,128)(2,1)} %uw_hbm.1, bf16[4,512,768]{2,1,0:T(8,128)(2,1)} %dw_hbm.1), custom_call_target="tpu_custom_call" | custom-call | tf_op jit(solution)/shard_map/pallas_call | solution.py:262
  136.8 1.6 %copy.8 = bf16[128,512]{1,0:T(8,128)(2,1)} copy(bf16[128,512]{1,0:T(8,128)(2,1)} %shard_map.64) | data formatting | bytes 262144
